TPU v7x, 32 devices: a whole 2x2x4 slice. The times are simulated.
32 devices in a mesh: row: 4 (over y, x), col: 8 (over z, core).
Axes of the slice: x: 2, y: 2, z: 4, core: 2. Of those that a mesh axis runs over, the one named last changes fastest.
Arguments:
- basis: bfloat16 [40, 131072], P(None, ('row', 'col'))
- expand: float32 [3, 8, 40], replicated, may hold values from -1 to 1
- tiles: bfloat16 [3, 3072, 128, 128], P(None, ('row', 'col')), may hold values from -0.3125 to 0.3125
- tile_rows: int32 [3072], P(('row', 'col')), may hold values from 0 to 255, as said below
- tile_cols: int32 [3072], P(('row', 'col')), may hold values from 0 to 127
Outputs:
- new_block: float32 [8, 131072], P(None, ('row', 'col'))
- coefficients: float32 [8, 40], replicated
- factor: float32 [8, 8], replicated
Inputs may be any that keep to these rules, and one draw needn't show every extreme that they name: `tile_rows`: each device's 96 tiles come in 8 runs of 12; the row tiles of run k are 12 distinct values from k * 32 to (k + 1) * 32 - 1.
All inputs are finite; a program needn't handle non-finite values.
Results may differ from a plain program's by a relative error of at most 0.0054.
Values may be sent and summed in bfloat16 or wider, within the bound.
A program may use at most 64 MiB of HBM per device.

v0:
```python
import math

import jax
import jax.numpy as jnp
from jax import lax
from jax.sharding import PartitionSpec as P


def shards(basis, expand, tiles, tile_rows, tile_cols):
    highest = lax.Precision.HIGHEST
    row_count = lax.axis_size("row")
    col_count = lax.axis_size("col")
    krylov, length = basis.shape
    tile_size = tiles.shape[2]
    block_size = expand.shape[1]
    entries = length * row_count * col_count
    inverse_root = 1.0 / math.sqrt(entries)
    region = length // tile_size
    basis_full = basis.astype(jnp.float32)
    series = jnp.einsum("mbk,kn->mbn", expand, basis_full, precision=highest).astype(jnp.bfloat16)
    gathered = lax.all_gather(series, "row", axis=2, tiled=True)
    col_tiles = gathered.reshape(3, block_size, row_count * length // tile_size, tile_size)
    picked = jnp.take(col_tiles, tile_cols, axis=2)
    products = jnp.einsum("mtij,mbtj->bti", tiles, picked, preferred_element_type=jnp.float32)
    slot_count = col_count * region
    onehot = (tile_rows[:, None] == jnp.arange(slot_count, dtype=jnp.int32)[None, :]).astype(
        jnp.float32
    )
    partial_value = jnp.einsum("ts,bti->bsi", onehot, products, precision=highest).reshape(
        block_size, slot_count * tile_size
    )
    applied = lax.psum_scatter(partial_value, "col", scatter_dimension=1, tiled=True)
    raw_proj = jnp.dot(applied, basis_full.T, precision=highest) * inverse_root
    correlation = jnp.dot(basis_full, basis_full.T, precision=highest) / entries
    energy = jnp.dot(applied, applied.T, precision=highest)
    first_pass, correlation, energy = lax.psum((raw_proj, correlation, energy), ("row", "col"))
    second_pass = first_pass - jnp.dot(first_pass, correlation, precision=highest)
    coefficients = first_pass + second_pass
    mixed = jnp.dot(first_pass, coefficients.T, precision=highest)
    curved = jnp.dot(
        jnp.dot(coefficients, correlation, precision=highest), coefficients.T, precision=highest
    )
    gram_block = (energy - mixed - mixed.T + curved) / entries
    cleaned = applied - jnp.dot(coefficients, basis_full, precision=highest) * inverse_root
    factor = jnp.linalg.cholesky(gram_block)
    new_block = lax.linalg.triangular_solve(factor, cleaned, left_side=True, lower=True)
    return (new_block, coefficients, factor)


def solution(mesh):
    return jax.shard_map(
        shards,
        mesh=mesh,
        in_specs=(
            P(None, ("row", "col")),
            P(),
            P(None, ("row", "col"), None, None),
            P(("row", "col")),
            P(("row", "col")),
        ),
        out_specs=(P(None, ("row", "col")), P(), P()),
        check_vma=False,
    )
```

profile of v0, /device:TPU:0, one launch (start us, length us, event | category | flops | bytes accessed | tf_op | source)
XLA Modules:
  0.0 118.4 jit_solution(17451722167365213223)
XLA Ops:
  7.2 0.0 copy-start
  7.2 0.0 copy-start.2
  7.2 0.0 reduce-scatter.2.cloned.1.call-start
  7.2 0.7 compare_select_fusion
  7.9 0.7 compare_and_fusion
  8.6 0.0 copy-done
  8.6 1.0 convolution_convert_fusion
  9.6 12.7 %all_gather.3 = bf16[3,8,16384]{2,1,0:T(8,128)(2,1)S(1)} all-gather(bf16[3,8,4096]{2,1,0:T(8,128)(2,1)S(1)} %convolution_convert_fusion), channel_id=1, replica_groups=mesh['row'=4,'col'=8] {'row'}, dimensions={2}, use_global_device_ids=true | all-gather | bytes 983040 | tf_op jit(solution)/shard_map/all_gather | solution.py:21
  22.3 0.8 gather_fusion
  23.1 5.9 %fusion = f32[96,8,128,1]{2,1,3,0:T(8,128)S(1)} fusion(bf16[3,96,128,128]{3,2,1,0:T(8,128)(2,1)} %param.7, bf16[96,3,8,128]{3,2,1,0:T(8,128)(2,1)S(1)} %gather_fusion, pred[96]{0:T(512)(128)(4,1)S(1)} %compare_and_fusion), kind=kOutput, calls=%fused_computation.1 | convolution fusion | flops 75792384 | bytes 10420320 | tf_op jit(solution)/shard_map/mtij,mbtj->bti/dot_general | solution.py:24
  29.0 0.0 copy-done.2
  29.0 0.7 convolution_bitcast_fusion
  29.7 0.3 copy.13
  30.0 1.6 %copy.31 = f32[1,8,256,128]{3,1,2,0:T(8,128)} copy(f32[1,8,256,128]{3,2,1,0:T(8,128)S(1)} %bitcast.54) | data formatting | bytes 2097152
  31.6 0.0 reduce-scatter.2.cloned.1.call-update
  31.6 0.2 convolution_multiply_fusion.1
  31.9 32.8 %reduce-scatter.2.cloned.1.call-done = f32[8,4096]{1,0:T(8,128)} async-done(((f32[8,32768]{1,0:T(8,128)}), f32[8,4096]{1,0:T(8,128)}) %reduce-scatter.2.cloned.1.call-update) | async-done | bytes 131088 | tf_op jit(solution)/shard_map/reduce_scatter | solution.py:32
  64.7 1.3 %convolution_multiply_fusion.2 = f32[8,40]{1,0:T(8,128)S(1)} fusion(f32[8,4096]{1,0:T(8,128)} %reduce-scatter.2.cloned.1.call-done, bf16[40,4096]{1,0:T(8,128)(2,1)S(1)} %copy-done), kind=kOutput, calls=%fused_computation.12 | convolution fusion | flops 15728960 | bytes 460032 | tf_op jit(solution)/shard_map/dot_general | solution.py:33
  66.0 1.3 %fusion.19 = f32[8,8]{0,1:T(8,128)S(1)} fusion(f32[8,4096]{1,0:T(8,128)} %reduce-scatter.2.cloned.1.call-done), kind=kOutput, calls=%fused_computation.39 | convolution fusion | flops 3145728 | bytes 131328 | tf_op jit(solution)/shard_map/dot_general | solution.py:35
  67.3 38.1 %all-reduce = (f32[8,40]{1,0:T(8,128)S(1)}, f32[40,40]{1,0:T(8,128)S(1)}, f32[8,8]{0,1:T(8,128)S(1)}) all-reduce(f32[8,40]{1,0:T(8,128)S(1)} %convolution_multiply_fusion.2, f32[40,40]{1,0:T(8,128)S(1)} %convolution_multiply_fusion.1, f32[8,8]{0,1:T(8,128)S(1)} %fusion.19), channel_id=1, replica_groups=mesh['row'=4,'col'=8] {'row','col'}, use_global_device_ids=true, to_apply=%region_2.3 | all-reduce | flops 1984 | bytes 15872 | tf_op jit(solution)/shard_map/psum | solution.py:36
  105.4 0.1 fusion.3
  105.5 0.0 copy-start.1
  105.5 0.1 fusion.20
  105.7 0.1 fusion.21
  105.8 0.1 copy.15
  105.9 0.1 fusion.4
  106.0 0.1 copy.17
  106.1 0.7 cholesky.16
  106.8 0.1 select_reduce_fusion
  106.9 0.6 compare_reduce_fusion
  107.5 1.2 %select_bitcast_fusion = (f32[1,8,8]{2,1,0:T(8,128)S(1)}, f32[8,8]{1,0:T(8,128)}) fusion(f32[8,8]{1,0:T(8,128)S(1)} %cholesky.16, pred[]{:T(512)} %compare_reduce_fusion), kind=kLoop, calls=%fused_computation.30 | loop fusion | flops 256 | bytes 769 | tf_op jit(solution)/shard_map/triangular_solve | solution.py:46
  108.7 0.6 custom-call.6
  109.4 1.2 fusion.2
  110.5 1.0 fusion.15
  111.5 0.0 copy-done.1
  (2 shorter events, 0.0 us)
Async XLA Ops:
  7.2 1.4 %copy-start = (bf16[40,4096]{1,0:T(8,128)(2,1)S(1)}, bf16[40,4096]{1,0:T(8,128)(2,1)}, u32[]{:S(2)}) copy-start(bf16[40,4096]{1,0:T(8,128)(2,1)} %param.5) | copy-start | bytes 983044
  7.2 21.8 %copy-start.2 = (s32[96]{0:T(128)S(1)}, s32[96]{0:T(128)}, u32[]{:S(2)}) copy-start(s32[96]{0:T(128)} %param.8) | copy-start | bytes 1156
  7.2 57.5 %reduce-scatter.2.cloned.1.call-start = ((), (), s32[]{:S(2)}) async-start(), calls=%async_computation.1 | async-start | bytes 1179648 | tf_op jit(solution)/shard_map/reduce_scatter | solution.py:32
  105.5 6.0 %copy-start.1 = (f32[8,40]{1,0:T(8,128)}, f32[8,40]{1,0:T(8,128)S(1)}, u32[]{:S(2)}) copy-start(f32[8,40]{1,0:T(8,128)S(1)} %fusion.3) | copy-start | bytes 3844
Sparse Core Ops, SparseCore 0:
  31.8 32.8 reduce-scatter.1
where the time goes:
time: 119 us; the launch traced here: 118 us
  blocking collectives  50.8 us (43%)
  waiting for transfers between devices  32.9 us (28%)
  between operations  14.1 us (12%)
  matrix products  13.1 us (11%)
  other arithmetic  4.65 us (4%)
  local copies, waits for them, and re-layouts  2.88 us (2%)
    psum x1, blocking collectives, shards(): lax.psum((raw_proj, correlation, energy), ('row', 'col'))  38.1 us
    reduce_scatter x1, waiting for transfers between devices, shards(): lax.psum_scatter(partial_value, 'col', scatter_dimension=1, tiled=True)  32.8 us
    all_gather x1, blocking collectives, shards(): gathered = lax.all_gather(series, 'row', axis=2, tiled=True)  12.7 us
    dot_general x1, matrix products, shards(): jnp.einsum('mtij,mbtj->bti', tiles, picked, preferred_element_type=jnp.fl...  5.9 us
  transfers between devices with their start and end apart: 1, of which 1 were waited for; matrix products, arithmetic and copies ran while one was open for 0% of the time, Pallas kernels for 0%

commit v1 on v0

v1 whole, which is shorter than its diff:
```python
import functools
import math

import jax
import jax.numpy as jnp
from jax import lax
from jax.experimental import pallas as pl
from jax.experimental.pallas import tpu as pltpu
from jax.sharding import PartitionSpec as P

F32 = jnp.float32
BF16 = jnp.bfloat16
NT = (((1,), (1,)), ((), ()))


def exact(a, b, dims=(((1,), (0,)), ((), ()))):
    return lax.dot_general(a, b, dims, precision=lax.Precision.HIGHEST, preferred_element_type=F32)


def pieces(x):
    one = x.astype(BF16).astype(F32)
    rest = x - one
    two = rest.astype(BF16).astype(F32)
    three = rest - two
    return jnp.concatenate([one, two, three], axis=0).astype(BF16)


def fold(x, rows):
    return x[:rows] + x[rows : 2 * rows] + x[2 * rows :]


def kernel(
    nrow,
    ncol,
    expand_ref,
    rows_ref,
    picks_ref,
    basis_hbm,
    tiles_hbm,
    new_ref,
    coef_ref,
    factor_ref,
    basis,
    tiles,
    cols,
    outbox,
    inbox,
    seg_out,
    seg_in,
    corr_col,
    corr_row,
    tail_col,
    tail_row,
    spread,
    app,
    basis_sem,
    tile_sem,
    ser_send,
    ser_recv,
    seg_send,
    seg_recv,
    box_send,
    box_recv,
    cc_send,
    cc_recv,
    cr_send,
    cr_recv,
    tc_send,
    tc_recv,
    tr_send,
    tr_recv,
):
    r = lax.axis_index("row")
    c = lax.axis_index("col")
    krylov, length = basis.shape
    kinds, tpd, tile, _ = tiles.shape
    cap = tpd // ncol
    region = length // tile
    bs = expand_ref.shape[1]
    entries = length * nrow * ncol
    inverse_root = 1.0 / math.sqrt(entries)
    width = seg_in.shape[2]

    load_basis = pltpu.make_async_copy(basis_hbm, basis, basis_sem)
    load_basis.start()

    def chunk_copy(m, k):
        part = pl.ds(k * cap, cap)
        return pltpu.make_async_copy(tiles_hbm.at[m, part], tiles.at[m, part], tile_sem.at[m, k])

    for j in range(1, ncol + 1):
        k = lax.rem(c + j, ncol)
        for m in range(kinds):
            chunk_copy(m, k).start()

    barrier = pltpu.get_barrier_semaphore()
    for j in range(1, nrow):
        pl.semaphore_signal(barrier, inc=1, device_id={"row": lax.rem(r + j, nrow)}, device_id_type=pl.DeviceIdType.MESH)
    for j in range(1, ncol):
        pl.semaphore_signal(barrier, inc=1, device_id={"col": lax.rem(c + j, ncol)}, device_id_type=pl.DeviceIdType.MESH)

    def remote(src, dst, send_sem, recv_sem, where):
        return pltpu.make_async_remote_copy(
            src_ref=src, dst_ref=dst, send_sem=send_sem, recv_sem=recv_sem,
            device_id=where, device_id_type=pl.DeviceIdType.MESH,
        )

    def row_at(j):
        peer = lax.rem(r + j, nrow)
        return peer, {"row": peer}

    def col_at(j):
        peer = lax.rem(c + j, ncol)
        return peer, {"col": peer}

    load_basis.wait()
    expand = pieces(expand_ref[...].reshape(kinds * bs, krylov))
    for l in range(region):
        part = fold(jnp.dot(expand, basis[:, l * tile : (l + 1) * tile], preferred_element_type=F32), kinds * bs)
        for m in range(kinds):
            cols[m, r * region + l] = part[m * bs : (m + 1) * bs].astype(BF16)

    pl.semaphore_wait(barrier, nrow + ncol - 2)

    def series_copy(m, owner, peer, where):
        block = cols.at[m, pl.ds(owner * region, region)]
        return remote(block, block, ser_send.at[m, peer], ser_recv.at[m, owner], where)

    for m in range(kinds):
        for j in range(1, nrow):
            peer, where = row_at(j)
            series_copy(m, r, peer, where).start()

    slot = lax.broadcasted_iota(jnp.int32, (1, width), 1)
    for k in range(ncol):
        line = jnp.zeros((1, width), jnp.int32)
        for t in range(cap):
            line = jnp.where(lax.rem(slot, cap) == t, rows_ref[k * cap + t], line)
        seg_out[k] = line
    for j in range(1, ncol):
        peer, where = col_at(j)
        remote(seg_out.at[peer], seg_in.at[c], seg_send.at[peer], seg_recv.at[c], where).start()
    seg_in[c] = seg_out[c]

    corr_col[c] = jnp.pad(
        lax.dot_general(basis[...], basis[...], NT, preferred_element_type=F32), ((0, 0), (0, 128 - krylov))
    )
    for j in range(1, ncol):
        peer, where = col_at(j)
        remote(corr_col.at[c], corr_col.at[c], cc_send.at[peer], cc_recv.at[c], where).start()

    for m in range(kinds):
        for j in range(1, nrow):
            peer, where = row_at(j)
            series_copy(m, peer, peer, where).wait_recv()

    def products(k, dst):
        for m in range(kinds):
            chunk_copy(m, k).wait()
        for t in range(cap):
            g = k * cap + t
            at = picks_ref[g]
            x = jnp.concatenate([cols[m, at] for m in range(kinds)], axis=1)
            w = jnp.concatenate([tiles[m, g] for m in range(kinds)], axis=1)
            dst[k, t] = lax.dot_general(x, w, NT, preferred_element_type=F32).astype(BF16)

    def box_copy(k, where):
        return remote(outbox.at[k], inbox.at[c], box_send.at[k], box_recv.at[c], where)

    def chunk(j, carry):
        k, where = col_at(j)
        products(k, outbox)
        box_copy(k, where).start()
        return carry

    lax.fori_loop(1, ncol, chunk, 0)
    products(c, inbox)

    for j in range(1, ncol):
        peer, where = col_at(j)
        remote(corr_col.at[c], corr_col.at[peer], cc_send.at[peer], cc_recv.at[peer], where).wait_recv()
    corr_row[r] = jnp.sum(corr_col[...], axis=0)
    for j in range(1, nrow):
        peer, where = row_at(j)
        remote(corr_row.at[r], corr_row.at[r], cr_send.at[peer], cr_recv.at[r], where).start()

    for j in range(1, ncol):
        peer, where = col_at(j)
        remote(seg_out.at[peer], seg_in.at[peer], seg_send.at[peer], seg_recv.at[peer], where).wait_recv()
    line = seg_in[0]
    for k in range(1, ncol):
        line = jnp.where(lax.div(slot, cap) == k, seg_in[k], line)
    here = lax.broadcasted_iota(jnp.int32, (region, tpd), 0) + c * region
    onehot = (line[:, :tpd] == here).astype(F32).astype(BF16)

    for j in range(1, nrow):
        peer, where = row_at(j)
        remote(corr_row.at[r], corr_row.at[peer], cr_send.at[peer], cr_recv.at[peer], where).wait_recv()
    corr = jnp.sum(corr_row[...], axis=0)[:, :krylov] / entries
    eye = (
        lax.broadcasted_iota(jnp.int32, (krylov, krylov), 0) == lax.broadcasted_iota(jnp.int32, (krylov, krylov), 1)
    ).astype(F32)
    once = eye - corr
    both = eye + once
    kern = exact(both, eye + exact(once, once))

    for j in range(1, ncol):
        peer, where = col_at(j)
        remote(outbox.at[peer], inbox.at[peer], box_send.at[peer], box_recv.at[peer], where).wait_recv()
    spread[...] = inbox[...].astype(F32).reshape(tpd, bs, tile)
    for b in range(bs):
        app[:, b, :] = jnp.dot(onehot, spread[:, b, :].astype(BF16), preferred_element_type=F32)
    applied = jnp.concatenate([app[s] for s in range(region)], axis=1)

    split = pieces(applied)
    raw = fold(lax.dot_general(split, basis[...], NT, preferred_element_type=F32), bs)
    energy = fold(lax.dot_general(split, split, NT, preferred_element_type=F32), bs)
    energy = energy[:, :bs] + energy[:, bs : 2 * bs] + energy[:, 2 * bs :]
    tail_col[c] = jnp.concatenate([raw, energy, jnp.zeros((bs, 128 - krylov - bs), F32)], axis=1)
    for j in range(1, ncol):
        peer, where = col_at(j)
        remote(tail_col.at[c], tail_col.at[c], tc_send.at[peer], tc_recv.at[c], where).start()
    for j in range(1, ncol):
        peer, where = col_at(j)
        remote(tail_col.at[c], tail_col.at[peer], tc_send.at[peer], tc_recv.at[peer], where).wait_recv()
    tail_row[r] = jnp.sum(tail_col[...], axis=0)
    for j in range(1, nrow):
        peer, where = row_at(j)
        remote(tail_row.at[r], tail_row.at[r], tr_send.at[peer], tr_recv.at[r], where).start()
    for j in range(1, nrow):
        peer, where = row_at(j)
        remote(tail_row.at[r], tail_row.at[peer], tr_send.at[peer], tr_recv.at[peer], where).wait_recv()
    total = jnp.sum(tail_row[...], axis=0)

    first = total[:, :krylov] * inverse_root
    coefficients = exact(first, both)
    gram = (total[:, krylov : krylov + bs] - exact(exact(first, kern), first, NT)) / entries
    coef_ref[...] = coefficients

    sub = lax.broadcasted_iota(jnp.int32, (bs, bs), 0)
    lane = lax.broadcasted_iota(jnp.int32, (bs, bs), 1)
    up = lax.broadcasted_iota(jnp.int32, (bs, 1), 0)
    factor = jnp.zeros((bs, bs), F32)
    inverse = jnp.zeros((bs, 1), F32)
    steps = []
    for j in range(bs):
        column, line = gram[:, j : j + 1], gram[j : j + 1, :]
        pivot = jnp.sqrt(gram[j : j + 1, j : j + 1])
        column = jnp.where(up >= j, column / pivot, 0.0)
        factor = jnp.where(lane == j, column, factor)
        inverse = jnp.where(up == j, 1.0 / pivot, inverse)
        steps.append(jnp.where(up > j, column, 0.0))
        gram = gram - column * (line / pivot)
    factor_ref[...] = factor

    cleaned = applied - fold(
        jnp.dot(pieces(coefficients * inverse_root), basis[...], preferred_element_type=F32), bs
    )
    solved = cleaned * inverse
    for j in range(bs - 1):
        solved = solved - (steps[j] * inverse) * solved[j : j + 1, :]
    new_ref[...] = solved

    for m in range(kinds):
        for j in range(1, nrow):
            peer, where = row_at(j)
            series_copy(m, r, peer, where).wait_send()
    for j in range(1, ncol):
        peer, where = col_at(j)
        remote(seg_out.at[peer], seg_in.at[c], seg_send.at[peer], seg_recv.at[c], where).wait_send()
        remote(corr_col.at[c], corr_col.at[c], cc_send.at[peer], cc_recv.at[c], where).wait_send()
        box_copy(peer, where).wait_send()
        remote(tail_col.at[c], tail_col.at[c], tc_send.at[peer], tc_recv.at[c], where).wait_send()
    for j in range(1, nrow):
        peer, where = row_at(j)
        remote(corr_row.at[r], corr_row.at[r], cr_send.at[peer], cr_recv.at[r], where).wait_send()
        remote(tail_row.at[r], tail_row.at[r], tr_send.at[peer], tr_recv.at[r], where).wait_send()


def shards(basis, expand, tiles, tile_rows, tile_cols):
    nrow = lax.axis_size("row")
    ncol = lax.axis_size("col")
    krylov, length = basis.shape
    kinds, tpd, tile, _ = tiles.shape
    bs = expand.shape[1]
    region = length // tile
    cap = tpd // ncol
    width = -(-tpd // 128) * 128
    dma = pltpu.SemaphoreType.DMA
    vmem, smem = pl.BlockSpec(memory_space=pltpu.VMEM), pl.BlockSpec(memory_space=pltpu.SMEM)
    hbm = pl.BlockSpec(memory_space=pl.ANY)
    return pl.pallas_call(
        functools.partial(kernel, nrow, ncol),
        out_shape=(
            jax.ShapeDtypeStruct((bs, length), F32),
            jax.ShapeDtypeStruct((bs, krylov), F32),
            jax.ShapeDtypeStruct((bs, bs), F32),
        ),
        in_specs=[vmem, smem, smem, hbm, hbm],
        out_specs=(vmem, vmem, vmem),
        scratch_shapes=[
            pltpu.VMEM((krylov, length), BF16),
            pltpu.VMEM((kinds, tpd, tile, tile), BF16),
            pltpu.VMEM((kinds, nrow * region, bs, tile), BF16),
            pltpu.VMEM((ncol, cap, bs, tile), BF16),
            pltpu.VMEM((ncol, cap, bs, tile), BF16),
            pltpu.VMEM((ncol, 1, width), jnp.int32),
            pltpu.VMEM((ncol, 1, width), jnp.int32),
            pltpu.VMEM((ncol, krylov, 128), F32),
            pltpu.VMEM((nrow, krylov, 128), F32),
            pltpu.VMEM((ncol, bs, 128), F32),
            pltpu.VMEM((nrow, bs, 128), F32),
            pltpu.VMEM((tpd, bs, tile), F32),
            pltpu.VMEM((region, bs, tile), F32),
            dma,
            dma((kinds, ncol)),
            dma((kinds, nrow)),
            dma((kinds, nrow)),
            dma((ncol,)),
            dma((ncol,)),
            dma((ncol,)),
            dma((ncol,)),
            dma((ncol,)),
            dma((ncol,)),
            dma((nrow,)),
            dma((nrow,)),
            dma((ncol,)),
            dma((ncol,)),
            dma((nrow,)),
            dma((nrow,)),
        ],
        compiler_params=pltpu.CompilerParams(
            collective_id=0, has_side_effects=True, vmem_limit_bytes=48 * 1024 * 1024
        ),
    )(expand, tile_rows, tile_cols, basis, tiles)


def solution(mesh):
    return jax.shard_map(
        shards,
        mesh=mesh,
        in_specs=(
            P(None, ("row", "col")),
            P(),
            P(None, ("row", "col"), None, None),
            P(("row", "col")),
            P(("row", "col")),
        ),
        out_specs=(P(None, ("row", "col")), P(), P()),
        check_vma=False,
    )
```

time: 119 us -> 39.6 us (0.33)
  blocking collectives: 50.8 us -> 0 us
  Pallas kernels: 0 us -> 33.9 us
  waiting for transfers between devices: 32.9 us -> 0 us
  between operations: 14.1 us -> 0.65 us
  matrix products: 13.1 us -> 0 us
  other arithmetic: 4.65 us -> 0 us
  local copies, waits for them, and re-layouts: 2.88 us -> 4.82 us
    psum x1 -> x0, blocking collectives: 38.1 us -> none  [shards(): lax.psum((raw_proj, correlation, energy), ('row', 'col'))]
    pallas_call x0 -> x1, Pallas kernels: none -> 33.9 us  [shards(): pl.pallas_call(functools.partial(kernel, nrow, ncol), out_shape=(jax.Shap...]
    reduce_scatter x1 -> x0, waiting for transfers between devices: 32.8 us -> none  [shards(): lax.psum_scatter(partial_value, 'col', scatter_dimension=1, tiled=True)]
    all_gather x1 -> x0, blocking collectives: 12.7 us -> none  [shards(): gathered = lax.all_gather(series, 'row', axis=2, tiled=True)]
    dot_general x11 -> x0, matrix products: 12.1 us -> none  [the longest x1 5.9 us: shards(): jnp.einsum('mtij,mbtj->bti', tiles, picked, preferred_element_type=jnp.fl...]
    another operation x5 -> x0, other arithmetic: 3.27 us -> none  [the longest x2 1.86 us: shards(): lax.linalg.triangular_solve(factor, cleaned, left_side=True, lower=True)]
    unnamed x7 -> x11, local copies, waits for them, and re-layouts: 1.62 us -> 4.82 us
  transfers between devices with their start and end apart: 1 -> 0, of which waited for: 1 -> 0; matrix products, arithmetic and copies ran while one was open for 0% -> 0% of each run, Pallas kernels for 0% -> 0%
where the time goes in v1:
time: 39.6 us; the launch traced here: 39.4 us
  Pallas kernels  33.9 us (86%)
  local copies, waits for them, and re-layouts  4.82 us (12%)
  between operations  0.65 us (2%)
    pallas_call x1, Pallas kernels, shards(): pl.pallas_call(functools.partial(kernel, nrow, ncol), out_shape=(jax.Shap...  33.9 us
    unnamed x11, local copies, waits for them, and re-layouts  4.82 us

profile of v1, /device:TPU:0, one launch (start us, length us, event | category | flops | bytes accessed | tf_op | source)
XLA Modules:
  0.0 39.4 jit_solution(7531665004125139815)
XLA Ops:
  0.6 0.0 copy-start
  0.6 1.0 %copy-done = bf16[40,4096]{1,0:T(8,128)(2,1)S(1)} copy-done((bf16[40,4096]{1,0:T(8,128)(2,1)S(1)}, bf16[40,4096]{1,0:T(8,128)(2,1)}, u32[]{:S(2)}) %copy-start) | copy-done | bytes 327704
  1.6 0.0 copy-start.1
  1.6 0.7 %copy-done.1 = f32[3,8,40]{2,1,0:T(8,128)S(1)} copy-done((f32[3,8,40]{2,1,0:T(8,128)S(1)}, f32[3,8,40]{2,1,0:T(8,128)}, u32[]{:S(2)}) %copy-start.1) | copy-done | bytes 3864
  2.3 0.0 copy-start.2
  2.3 0.7 %copy-done.2 = s32[96]{0:T(128)S(1)} copy-done((s32[96]{0:T(128)S(1)}, s32[96]{0:T(128)}, u32[]{:S(2)}) %copy-start.2) | copy-done | bytes 408
  3.0 0.0 copy-start.3
  3.0 0.7 %copy-done.3 = s32[96]{0:T(128)S(1)} copy-done((s32[96]{0:T(128)S(1)}, s32[96]{0:T(128)}, u32[]{:S(2)}) %copy-start.3) | copy-done | bytes 408
  3.6 33.9 %shard_map.76 = (f32[8,4096]{1,0:T(8,128)S(1)}, f32[8,40]{1,0:T(8,128)S(1)}, f32[8,8]{1,0:T(8,128)S(1)}) custom-call(f32[3,8,40]{2,1,0:T(8,128)S(1)} %copy-done.1, s32[96]{0:T(128)S(1)} %copy-done.2, s32[96]{0:T(128)S(1)} %copy-done.3, bf16[40,4096]{1,0:T(8,128)(2,1)S(1)} %copy-done, bf16[3,96,128,128]{3,2,1,0:T(8,128)(2,1)} %tiles_hbm.1), custom_call_target="tpu_custom_call" | custom-call | tf_op jit(solution)/shard_map/pallas_call | solution.py:292
  37.5 0.7 %copy.11 = f32[8,4096]{1,0:T(8,128)} copy(f32[8,4096]{1,0:T(8,128)S(1)} %get-tuple-element.6) | data formatting | bytes 262144
  38.2 0.6 %copy.12 = f32[8,40]{1,0:T(8,128)} copy(f32[8,40]{1,0:T(8,128)S(1)} %get-tuple-element.7) | data formatting | bytes 2560
  38.8 0.6 %copy.13 = f32[8,8]{1,0:T(8,128)} copy(f32[8,8]{1,0:T(8,128)S(1)} %get-tuple-element.8) | data formatting | bytes 512
Async XLA Ops:
  0.6 1.0 %copy-start = (bf16[40,4096]{1,0:T(8,128)(2,1)S(1)}, bf16[40,4096]{1,0:T(8,128)(2,1)}, u32[]{:S(2)}) copy-start(bf16[40,4096]{1,0:T(8,128)(2,1)} %basis_hbm.1) | copy-start | bytes 983044
  1.6 0.7 %copy-start.1 = (f32[3,8,40]{2,1,0:T(8,128)S(1)}, f32[3,8,40]{2,1,0:T(8,128)}, u32[]{:S(2)}) copy-start(f32[3,8,40]{2,1,0:T(8,128)} %expand_ref.1) | copy-start | bytes 11524
  2.3 0.7 %copy-start.2 = (s32[96]{0:T(128)S(1)}, s32[96]{0:T(128)}, u32[]{:S(2)}) copy-start(s32[96]{0:T(128)} %rows_ref.1) | copy-start | bytes 1156
  3.0 0.7 %copy-start.3 = (s32[96]{0:T(128)S(1)}, s32[96]{0:T(128)}, u32[]{:S(2)}) copy-start(s32[96]{0:T(128)} %picks_ref.1) | copy-start | bytes 1156

commit v2 on v1

--- a/solution.py
+++ b/solution.py
@@ -32,14 +32,17 @@
 def kernel(
     nrow,
     ncol,
-    expand_ref,
-    rows_ref,
-    picks_ref,
+    expand_hbm,
+    rows_hbm,
+    picks_hbm,
     basis_hbm,
     tiles_hbm,
     new_ref,
     coef_ref,
     factor_ref,
+    expand_ref,
+    rows_ref,
+    picks_ref,
     basis,
     tiles,
     cols,
@@ -53,10 +56,13 @@
     tail_row,
     spread,
     app,
+    small_sem,
     basis_sem,
     tile_sem,
     ser_send,
     ser_recv,
+    fwd_send,
+    fwd_recv,
     seg_send,
     seg_recv,
     box_send,
@@ -83,6 +89,12 @@
 
     load_basis = pltpu.make_async_copy(basis_hbm, basis, basis_sem)
     load_basis.start()
+    small = [
+        pltpu.make_async_copy(src, dst, small_sem.at[i])
+        for i, (src, dst) in enumerate(((expand_hbm, expand_ref), (rows_hbm, rows_ref), (picks_hbm, picks_ref)))
+    ]
+    for copy in small:
+        copy.start()
 
     def chunk_copy(m, k):
         part = pl.ds(k * cap, cap)
@@ -113,6 +125,8 @@
         peer = lax.rem(c + j, ncol)
         return peer, {"col": peer}
 
+    for copy in small:
+        copy.wait()
     load_basis.wait()
     expand = pieces(expand_ref[...].reshape(kinds * bs, krylov))
     for l in range(region):
@@ -122,14 +136,24 @@
 
     pl.semaphore_wait(barrier, nrow + ncol - 2)
 
-    def series_copy(m, owner, peer, where):
+    outer = nrow // 2
+    side, pair = lax.rem(r, 2), lax.div(r, 2)
+    mate = r + 1 - 2 * side
+    others = [2 * lax.rem(pair + j, outer) + side for j in range(1, outer)]
+    half = region // 2
+
+    def series_copy(m, owner, peer):
         block = cols.at[m, pl.ds(owner * region, region)]
-        return remote(block, block, ser_send.at[m, peer], ser_recv.at[m, owner], where)
-
+        return remote(block, block, ser_send.at[m, peer], ser_recv.at[m, owner], {"row": peer})
+
+    def pass_on(m, owner, h, peer, slot):
+        block = cols.at[m, pl.ds(owner * region + h * half, half)]
+        return remote(block, block, fwd_send.at[m, slot, h], fwd_recv.at[m, owner, h], {"row": peer})
+
+    direct = [mate] + others
     for m in range(kinds):
-        for j in range(1, nrow):
-            peer, where = row_at(j)
-            series_copy(m, r, peer, where).start()
+        for peer in direct:
+            series_copy(m, r, peer).start()
 
     slot = lax.broadcasted_iota(jnp.int32, (1, width), 1)
     for k in range(ncol):
@@ -142,17 +166,43 @@
         remote(seg_out.at[peer], seg_in.at[c], seg_send.at[peer], seg_recv.at[c], where).start()
     seg_in[c] = seg_out[c]
 
-    corr_col[c] = jnp.pad(
-        lax.dot_general(basis[...], basis[...], NT, preferred_element_type=F32), ((0, 0), (0, 128 - krylov))
+    corr = lax.dot_general(basis[...], basis[...], NT, preferred_element_type=F32)
+    band = corr_col.shape[1]
+    lanes = corr_col.shape[2]
+    folds = -(-krylov // band)
+    corr = jnp.pad(corr, ((0, folds * band - krylov), (0, 0)))
+    corr_col[c] = jnp.concatenate(
+        [corr[i * band : (i + 1) * band] for i in range(folds)] + [jnp.zeros((band, lanes - folds * krylov), F32)], axis=1
     )
     for j in range(1, ncol):
         peer, where = col_at(j)
         remote(corr_col.at[c], corr_col.at[c], cc_send.at[peer], cc_recv.at[c], where).start()
 
+    def relay(m):
+        series_copy(m, mate, mate).wait_recv()
+        for other in others:
+            pass_on(m, mate, 1, other, other).start()
+        for other in others:
+            series_copy(m, other, other).wait_recv()
+            pass_on(m, other, 0, mate, other).start()
+
+    def relayed(m):
+        for other in others:
+            far = other + 1 - 2 * side
+            pass_on(m, far, 0, mate, far).wait_recv()
+            pass_on(m, far, 1, other, far).wait_recv()
+
     for m in range(kinds):
-        for j in range(1, nrow):
-            peer, where = row_at(j)
-            series_copy(m, peer, peer, where).wait_recv()
+        relay(m)
+    for j in range(1, ncol):
+        peer, where = col_at(j)
+        remote(corr_col.at[c], corr_col.at[peer], cc_send.at[peer], cc_recv.at[peer], where).wait_recv()
+    corr_row[r] = jnp.sum(corr_col[...], axis=0)
+    for j in range(1, nrow):
+        peer, where = row_at(j)
+        remote(corr_row.at[r], corr_row.at[r], cr_send.at[peer], cr_recv.at[r], where).start()
+    for m in range(kinds):
+        relayed(m)
 
     def products(k, dst):
         for m in range(kinds):
@@ -178,14 +228,6 @@
 
     for j in range(1, ncol):
         peer, where = col_at(j)
-        remote(corr_col.at[c], corr_col.at[peer], cc_send.at[peer], cc_recv.at[peer], where).wait_recv()
-    corr_row[r] = jnp.sum(corr_col[...], axis=0)
-    for j in range(1, nrow):
-        peer, where = row_at(j)
-        remote(corr_row.at[r], corr_row.at[r], cr_send.at[peer], cr_recv.at[r], where).start()
-
-    for j in range(1, ncol):
-        peer, where = col_at(j)
         remote(seg_out.at[peer], seg_in.at[peer], seg_send.at[peer], seg_recv.at[peer], where).wait_recv()
     line = seg_in[0]
     for k in range(1, ncol):
@@ -196,7 +238,8 @@
     for j in range(1, nrow):
         peer, where = row_at(j)
         remote(corr_row.at[r], corr_row.at[peer], cr_send.at[peer], cr_recv.at[peer], where).wait_recv()
-    corr = jnp.sum(corr_row[...], axis=0)[:, :krylov] / entries
+    corr = jnp.sum(corr_row[...], axis=0) / entries
+    corr = jnp.concatenate([corr[:, i * krylov : (i + 1) * krylov] for i in range(folds)], axis=0)[:krylov]
     eye = (
         lax.broadcasted_iota(jnp.int32, (krylov, krylov), 0) == lax.broadcasted_iota(jnp.int32, (krylov, krylov), 1)
     ).astype(F32)
@@ -262,9 +305,11 @@
     new_ref[...] = solved
 
     for m in range(kinds):
-        for j in range(1, nrow):
-            peer, where = row_at(j)
-            series_copy(m, r, peer, where).wait_send()
+        for peer in direct:
+            series_copy(m, r, peer).wait_send()
+        for other in others:
+            pass_on(m, mate, 1, other, other).wait_send()
+            pass_on(m, other, 0, mate, other).wait_send()
     for j in range(1, ncol):
         peer, where = col_at(j)
         remote(seg_out.at[peer], seg_in.at[c], seg_send.at[peer], seg_recv.at[c], where).wait_send()
@@ -287,8 +332,9 @@
     cap = tpd // ncol
     width = -(-tpd // 128) * 128
     dma = pltpu.SemaphoreType.DMA
-    vmem, smem = pl.BlockSpec(memory_space=pltpu.VMEM), pl.BlockSpec(memory_space=pltpu.SMEM)
-    hbm = pl.BlockSpec(memory_space=pl.ANY)
+    band = 16
+    lanes = -(-(-(-krylov // band) * krylov) // 128) * 128
+    vmem, hbm = pl.BlockSpec(memory_space=pltpu.VMEM), pl.BlockSpec(memory_space=pltpu.HBM)
     return pl.pallas_call(
         functools.partial(kernel, nrow, ncol),
         out_shape=(
@@ -296,9 +342,12 @@
             jax.ShapeDtypeStruct((bs, krylov), F32),
             jax.ShapeDtypeStruct((bs, bs), F32),
         ),
-        in_specs=[vmem, smem, smem, hbm, hbm],
+        in_specs=[hbm] * 5,
         out_specs=(vmem, vmem, vmem),
         scratch_shapes=[
+            pltpu.VMEM(expand.shape, F32),
+            pltpu.SMEM((tpd,), jnp.int32),
+            pltpu.SMEM((tpd,), jnp.int32),
             pltpu.VMEM((krylov, length), BF16),
             pltpu.VMEM((kinds, tpd, tile, tile), BF16),
             pltpu.VMEM((kinds, nrow * region, bs, tile), BF16),
@@ -306,16 +355,19 @@
             pltpu.VMEM((ncol, cap, bs, tile), BF16),
             pltpu.VMEM((ncol, 1, width), jnp.int32),
             pltpu.VMEM((ncol, 1, width), jnp.int32),
-            pltpu.VMEM((ncol, krylov, 128), F32),
-            pltpu.VMEM((nrow, krylov, 128), F32),
+            pltpu.VMEM((ncol, band, lanes), F32),
+            pltpu.VMEM((nrow, band, lanes), F32),
             pltpu.VMEM((ncol, bs, 128), F32),
             pltpu.VMEM((nrow, bs, 128), F32),
             pltpu.VMEM((tpd, bs, tile), F32),
             pltpu.VMEM((region, bs, tile), F32),
+            dma((3,)),
             dma,
             dma((kinds, ncol)),
             dma((kinds, nrow)),
             dma((kinds, nrow)),
+            dma((kinds, nrow, 2)),
+            dma((kinds, nrow, 2)),
             dma((ncol,)),
             dma((ncol,)),
             dma((ncol,)),
@@ -332,7 +384,7 @@
         compiler_params=pltpu.CompilerParams(
             collective_id=0, has_side_effects=True, vmem_limit_bytes=48 * 1024 * 1024
         ),
-    )(expand, tile_rows, tile_cols, basis, tiles)
+    )(*(pltpu.with_memory_space_constraint(x, pltpu.HBM) for x in (expand, tile_rows, tile_cols, basis, tiles)))
 
 
 def solution(mesh):

time: 39.6 us -> 36.8 us (0.929)
  local copies, waits for them, and re-layouts: 4.82 us -> 1.84 us
    unnamed x11 -> x3, local copies, waits for them, and re-layouts: 4.82 us -> 1.84 us
where the time goes in v2:
time: 36.8 us; the launch traced here: 36.5 us
  Pallas kernels  34 us (92%)
  local copies, waits for them, and re-layouts  1.84 us (5%)
  between operations  0.64 us (2%)
    pallas_call x1, Pallas kernels, shards(): pl.pallas_call(functools.partial(kernel, nrow, ncol), out_shape=(jax.Shap...  34 us
    unnamed x3, local copies, waits for them, and re-layouts  1.84 us

profile of v2, /device:TPU:0, one launch (start us, length us, event | category | flops | bytes accessed | tf_op | source)
XLA Modules:
  0.0 36.5 jit_solution(925287348055365405)
XLA Ops:
  0.6 34.0 %shard_map.76 = (f32[8,4096]{1,0:T(8,128)S(1)}, f32[8,40]{1,0:T(8,128)S(1)}, f32[8,8]{1,0:T(8,128)S(1)}) custom-call(f32[3,8,40]{2,1,0:T(8,128)} %expand_hbm.1, s32[96]{0:T(128)} %rows_hbm.1, s32[96]{0:T(128)} %picks_hbm.1, bf16[40,4096]{1,0:T(8,128)(2,1)} %basis_hbm.1, bf16[3,96,128,128]{3,2,1,0:T(8,128)(2,1)} %tiles_hbm.1), custom_call_target="tpu_custom_call" | custom-call | tf_op jit(solution)/shard_map/pallas_call | solution.py:338
  34.7 0.7 %copy.11 = f32[8,4096]{1,0:T(8,128)} copy(f32[8,4096]{1,0:T(8,128)S(1)} %get-tuple-element.6) | data formatting | bytes 262144
  35.3 0.6 %copy.12 = f32[8,40]{1,0:T(8,128)} copy(f32[8,40]{1,0:T(8,128)S(1)} %get-tuple-element.7) | data formatting | bytes 2560
  35.9 0.6 %copy.13 = f32[8,8]{1,0:T(8,128)} copy(f32[8,8]{1,0:T(8,128)S(1)} %get-tuple-element.8) | data formatting | bytes 512
